TPU v7x, 32 devices: a whole 2x2x4 slice. The times are simulated.
32 devices in a mesh: up: 8 (over y, x, core), dn: 4 (over z).
Axes of the slice: x: 2, y: 2, z: 4, core: 2. Of those that a mesh axis runs over, the one named last changes fastest.
Arguments:
- start_vector: bfloat16 [13312, 13312], P('up', 'dn'), may hold values from -6 to 6
- hop_tiles: bfloat16 [104, 5, 128, 128], replicated, may hold values from -0.5 to 0.5
- tile_columns: int32 [104, 5], replicated, may hold values from 0 to 103, as said below
- tile_signs: int32 [104, 5], replicated, may hold values from 0 to 1
- occupation: int32 [16, 13312], replicated, may hold values from 0 to 1, as said below
Outputs:
- next_vector: bfloat16 [13312, 13312], P('up', 'dn')
- alphas: float32 [2], replicated
- betas: float32 [2], replicated
Inputs may be any that keep to these rules, and one draw needn't show every extreme that they name: Each row of tile_columns names 5 different tile columns. Every column of occupation holds exactly 8 ones.
All inputs are finite; a program needn't handle non-finite values.
Results may differ from a plain program's by a relative error of at most 0.0065.
Values may be sent and summed in bfloat16 or wider, within the bound.
A program may use at most 256 MiB of HBM per device.

v0:
```python
import jax
import jax.numpy as jnp
from jax import lax
from jax.sharding import PartitionSpec as P

STEPS = 2


coupling = 4.0


def hop_lead(matrix, signed, tile_columns):
    layout = matrix.shape
    tile_width = signed.shape[-1]
    cube = matrix.reshape(layout[0] // tile_width, tile_width, -1)
    picked = cube[tile_columns]
    result = jnp.einsum("ikab,ikbm->iam", signed, picked, preferred_element_type=jnp.float32)
    return result.reshape(layout).astype(jnp.bfloat16)


def body(start_vector, hop_tiles, tile_columns, tile_signs, occupation):
    signed = hop_tiles * (1 - 2 * tile_signs).astype(jnp.bfloat16)[:, :, None, None]
    rows_local, cols_local = start_vector.shape
    count_up = lax.axis_size("up")
    count_down = lax.axis_size("dn")
    row_start = lax.axis_index("up") * rows_local
    col_start = lax.axis_index("dn") * cols_local
    block_rows, block_cols = start_vector.shape
    occ_rows = lax.dynamic_slice_in_dim(occupation, row_start, block_rows, 1).astype(jnp.bfloat16)
    occ_cols = lax.dynamic_slice_in_dim(occupation, col_start, block_cols, 1).astype(jnp.bfloat16)
    diagonal = coupling * jnp.einsum(
        "sa,sb->ab", occ_rows, occ_cols, preferred_element_type=jnp.float32
    )
    vector = start_vector.astype(jnp.float32)
    total = lax.psum(jnp.sum(vector * vector), ("up", "dn"))
    vector = vector / jnp.maximum(jnp.sqrt(total), 1.0)
    length = total / jnp.maximum(total, 1.0)
    previous = jnp.zeros_like(vector)
    beta_value = jnp.float32(0.0)
    alpha_list = []
    beta_list = []
    for iteration in range(STEPS):
        rounded = vector.astype(jnp.bfloat16)
        cube = rounded.reshape(block_rows, count_up, block_cols // count_up)
        up_part = lax.all_to_all(cube, "up", split_axis=1, concat_axis=0, tiled=True)
        up_whole = up_part.reshape(up_part.shape[0], up_part.shape[2])
        up_hopped = hop_lead(up_whole, signed, tile_columns).reshape(up_part.shape)
        moved = lax.all_to_all(up_hopped, "up", split_axis=0, concat_axis=1, tiled=True)
        hopped_up = moved.reshape(block_rows, block_cols)
        flipped = rounded.T.reshape(block_cols, count_down, block_rows // count_down)
        part = lax.all_to_all(flipped, "dn", split_axis=1, concat_axis=0, tiled=True)
        whole = part.reshape(part.shape[0], part.shape[2])
        hopped = hop_lead(whole, signed, tile_columns).reshape(part.shape)
        returned = lax.all_to_all(hopped, "dn", split_axis=0, concat_axis=1, tiled=True)
        hopped_down = returned.reshape(block_cols, block_rows).T
        work = (
            hopped_up.astype(jnp.float32)
            + hopped_down.astype(jnp.float32)
            + diagonal * vector
            - beta_value * previous
        )
        intersect, square = lax.psum((jnp.sum(work * vector), jnp.sum(work * work)), ("up", "dn"))
        work = work - intersect * vector
        residual = square - 2.0 * intersect * intersect + intersect * intersect * length
        beta_value = jnp.sqrt(jnp.maximum(residual, 1.0))
        length = residual / jnp.maximum(residual, 1.0)
        previous = vector
        vector = work / beta_value
        alpha_list.append(intersect)
        beta_list.append(beta_value)
    final = vector.astype(jnp.bfloat16)
    return (final, jnp.stack(alpha_list), jnp.stack(beta_list))


def solution(mesh):
    placed = (P("up", "dn"), P(), P(), P(), P())
    return jax.shard_map(
        body, mesh=mesh, in_specs=placed, out_specs=(P("up", "dn"), P(), P()), check_vma=False
    )
```

profile of v0, /device:TPU:12, one launch (start us, length us, event | category | flops | bytes accessed | tf_op | source)
XLA Modules:
  0.0 2605.1 jit_solution(15196336587195113989)
XLA Ops:
  11.1 41.6 %psum.35 = f32[]{:T(128)} all-reduce(f32[]{:T(128)} %fusion), channel_id=1, replica_groups=mesh['up'=8,'dn'=4] {'up','dn'}, use_global_device_ids=true, to_apply=%region_1.0 | all-reduce | flops 1 | bytes 8 | tf_op jit(solution)/shard_map/psum | solution.py:35
  80.3 127.1 %all_to_all.96 = bf16[1664,8,416]{0,2,1:T(8,128)(2,1)} all-to-all(bf16[1664,8,416]{0,2,1:T(8,128)(2,1)} %bitcast.112), channel_id=1, replica_groups=mesh['up'=8,'dn'=4] {'up'}, dimensions={1} | all-to-all | bytes 22151168 | tf_op jit(solution)/shard_map/all_to_all | solution.py:45
  291.6 29.5 %bitcast_convert_fusion.3 = bf16[104,128,416]{1,2,0:T(8,128)(2,1)} fusion(bf16[104,5,128,416]{2,3,1,0:T(8,128)(2,1)} %bitcast.107, bf16[104,5,128,128]{3,2,1,0:T(8,128)(2,1)} %param.6, bf16[104,5]{1,0:T(8,128)(2,1)S(1)} %copy.61), kind=kOutput, calls=%fused_computation.15 | convolution fusion | flops 7102431232 | bytes 83493904 | tf_op jit(solution)/shard_map/ikab,ikbm->iam/dot_general | solution.py:17
  337.4 77.7 %reshape.155 = bf16[13312,1,416]{2,1,0:T(2,128)(2,1)} reshape(bf16[104,128,416]{2,1,0:T(8,128)(2,1)} %copy.95) | data formatting | bytes 22151168 | tf_op jit(solution)/shard_map/convert_element_type | solution.py:18
  415.7 87.5 %reduce = bf16[13312,416]{1,0:T(8,128)(2,1)} reduce(bf16[13312,1,416]{2,1,0:T(2,128)(2,1)} %reshape.155, bf16[]{:T(256)} %broadcast.21), dimensions={1}, to_apply=%reshape.155.reduce_sub_computation | reduce | bytes 22151170 | tf_op jit(solution)/shard_map/convert_element_type | solution.py:18
  587.4 26.5 %gather_fusion.1 = bf16[520,128,416]{1,2,0:T(8,128)(2,1)} fusion(bf16[104,128,416]{1,2,0:T(8,128)(2,1)} %copy.71, s32[1024]{0:T(1024)S(1)} %pad_clamp_fusion), kind=kCustom, calls=%fused_computation.1 | custom fusion | bytes 110757920 | tf_op jit(solution)/shard_map/gather | solution.py:16
  613.9 29.4 %bitcast_convert_fusion.2 = bf16[104,128,416]{1,2,0:T(8,128)(2,1)} fusion(bf16[104,5,128,416]{2,3,1,0:T(8,128)(2,1)} %bitcast.108, bf16[104,5,128,128]{3,2,1,0:T(8,128)(2,1)} %param.6, bf16[104,5]{1,0:T(8,128)(2,1)S(1)} %copy.61), kind=kOutput, calls=%fused_computation.14 | convolution fusion | flops 7102431232 | bytes 83493904 | tf_op jit(solution)/shard_map/ikab,ikbm->iam/dot_general | solution.py:17
  659.6 77.6 %reshape.156 = bf16[13312,1,416]{2,1,0:T(2,128)(2,1)} reshape(bf16[104,128,416]{2,1,0:T(8,128)(2,1)} %copy.96) | data formatting | bytes 22151168 | tf_op jit(solution)/shard_map/convert_element_type | solution.py:18
  737.2 87.6 %reduce.1 = bf16[13312,416]{1,0:T(8,128)(2,1)} reduce(bf16[13312,1,416]{2,1,0:T(2,128)(2,1)} %reshape.156, bf16[]{:T(256)} %broadcast.21), dimensions={1}, to_apply=%reshape.156.reduce_sub_computation | reduce | bytes 22151170 | tf_op jit(solution)/shard_map/convert_element_type | solution.py:18
  854.9 30.4 %reshape.160 = bf16[13312,1,416]{2,1,0:T(2,128)(2,1)} reshape(bf16[8,2,346112]{2,1,0:T(2,128)(2,1)} %all-to-all-done.1) | data formatting | bytes 22151168
  885.3 52.5 %copy.68 = bf16[13312,1,416]{0,2,1:T(8,128)(2,1)} copy(bf16[13312,1,416]{2,1,0:T(2,128)(2,1)} %reshape.160) | data formatting | bytes 22151168 | tf_op jit(solution)/shard_map/all_to_all | solution.py:48
  995.3 96.4 %all-to-all-done.3 = bf16[4,2,692224]{2,1,0:T(2,128)(2,1)} async-done(((bf16[4,2,692224]{2,1,0:T(2,128)(2,1)}), bf16[4,2,692224]{2,1,0:T(2,128)(2,1)}, u32[]{:S(2)}, u32[]{:S(2)}) %all-to-all-start.3) | async-done | bytes 11075616 | tf_op jit(solution)/shard_map/all_to_all | solution.py:54
  1091.7 45.3 %reshape.162 = bf16[13312,1,416]{2,1,0:T(2,128)(2,1)} reshape(bf16[4,2,692224]{2,1,0:T(2,128)(2,1)} %all-to-all-done.3) | data formatting | bytes 22151168
  1137.0 52.8 %copy.74 = bf16[13312,1,416]{0,2,1:T(8,128)(2,1)} copy(bf16[13312,1,416]{2,1,0:T(2,128)(2,1)} %reshape.162) | data formatting | bytes 22151168 | tf_op jit(solution)/shard_map/all_to_all | solution.py:54
  1230.8 32.3 %multiply_reduce_fusion.3 = (f32[]{:T(128)}, f32[]{:T(128)}, f32[1664,3328]{1,0:T(8,128)}, f32[1664,3328]{1,0:T(8,128)}) fusion(f32[]{:T(128)S(6)} %max.13, bf16[1664,3328]{1,0:T(8,128)(2,1)} %param.5, f32[1664,3328]{1,0:T(8,128)} %copy.76, f32[3328,4,1,416]{0,3,1,2:T(8,128)} %copy.75, s32[16,13312]{1,0:T(8,128)} %param.9, s32[]{:T(128)S(6)} %select_n.14, ...), kind=kOutput, calls=%fused_computation.21 | convolution fusion | flops 232667136 | bytes 99999760 | tf_op jit(solution)/shard_map/sa,sb->ab/dot_general | solution.py:31
  1263.1 43.3 %all-reduce.1 = (f32[]{:T(128)}, f32[]{:T(128)}) all-reduce(f32[]{:T(128)} %get-tuple-element.6, f32[]{:T(128)} %get-tuple-element.5), channel_id=1, replica_groups=mesh['up'=8,'dn'=4] {'up','dn'}, use_global_device_ids=true, to_apply=%region_5.0 | all-reduce | flops 2 | bytes 16 | tf_op jit(solution)/shard_map/psum | solution.py:62
  1348.6 127.0 %all_to_all.97 = bf16[1664,8,416]{0,2,1:T(8,128)(2,1)} all-to-all(bf16[1664,8,416]{0,2,1:T(8,128)(2,1)} %bitcast.113), channel_id=1, replica_groups=mesh['up'=8,'dn'=4] {'up'}, dimensions={1} | all-to-all | bytes 22151168 | tf_op jit(solution)/shard_map/all_to_all | solution.py:45
  1532.4 26.5 %gather_fusion.2 = bf16[520,128,416]{1,2,0:T(8,128)(2,1)} fusion(bf16[104,128,416]{1,2,0:T(8,128)(2,1)} %copy.79, s32[1024]{0:T(1024)S(1)} %copy-done.1), kind=kCustom, calls=%fused_computation.2 | custom fusion | bytes 110757920 | tf_op jit(solution)/shard_map/gather | solution.py:16
  1558.9 29.4 %bitcast_convert_fusion.1 = bf16[104,128,416]{1,2,0:T(8,128)(2,1)} fusion(bf16[104,5,128,416]{2,3,1,0:T(8,128)(2,1)} %bitcast.109, bf16[104,5,128,128]{3,2,1,0:T(8,128)(2,1)} %param.6, bf16[104,5]{1,0:T(8,128)(2,1)S(1)} %copy-done.3), kind=kOutput, calls=%fused_computation.13 | convolution fusion | flops 7102431232 | bytes 83493904 | tf_op jit(solution)/shard_map/ikab,ikbm->iam/dot_general | solution.py:17
  1604.6 77.7 %reshape.157 = bf16[13312,1,416]{2,1,0:T(2,128)(2,1)} reshape(bf16[104,128,416]{2,1,0:T(8,128)(2,1)} %copy.97) | data formatting | bytes 22151168 | tf_op jit(solution)/shard_map/convert_element_type | solution.py:18
  1682.3 87.5 %reduce.2 = bf16[13312,416]{1,0:T(8,128)(2,1)} reduce(bf16[13312,1,416]{2,1,0:T(2,128)(2,1)} %reshape.157, bf16[]{:T(256)} %broadcast.21), dimensions={1}, to_apply=%reshape.157.reduce_sub_computation | reduce | bytes 22151170 | tf_op jit(solution)/shard_map/convert_element_type | solution.py:18
  1854.0 26.5 %gather_fusion.3 = bf16[520,128,416]{1,2,0:T(8,128)(2,1)} fusion(bf16[104,128,416]{1,2,0:T(8,128)(2,1)} %copy.85, s32[1024]{0:T(1024)S(1)} %copy-done.1), kind=kCustom, calls=%fused_computation.3 | custom fusion | bytes 110757920 | tf_op jit(solution)/shard_map/gather | solution.py:16
  1880.5 29.4 %bitcast_convert_fusion = bf16[104,128,416]{1,2,0:T(8,128)(2,1)} fusion(bf16[104,5,128,416]{2,3,1,0:T(8,128)(2,1)} %bitcast.106, bf16[104,5,128,128]{3,2,1,0:T(8,128)(2,1)} %param.6, bf16[104,5]{1,0:T(8,128)(2,1)S(1)} %copy-done.3), kind=kOutput, calls=%fused_computation.12 | convolution fusion | flops 7102431232 | bytes 83493904 | tf_op jit(solution)/shard_map/ikab,ikbm->iam/dot_general | solution.py:17
  1926.3 77.6 %reshape.158 = bf16[13312,1,416]{2,1,0:T(2,128)(2,1)} reshape(bf16[104,128,416]{2,1,0:T(8,128)(2,1)} %copy.98) | data formatting | bytes 22151168 | tf_op jit(solution)/shard_map/convert_element_type | solution.py:18
  2003.8 87.6 %reduce.3 = bf16[13312,416]{1,0:T(8,128)(2,1)} reduce(bf16[13312,1,416]{2,1,0:T(2,128)(2,1)} %reshape.158, bf16[]{:T(256)} %broadcast.21), dimensions={1}, to_apply=%reshape.158.reduce_sub_computation | reduce | bytes 22151170 | tf_op jit(solution)/shard_map/convert_element_type | solution.py:18
  2120.2 30.4 %reshape.164 = bf16[13312,1,416]{2,1,0:T(2,128)(2,1)} reshape(bf16[8,2,346112]{2,1,0:T(2,128)(2,1)} %all-to-all-done.5) | data formatting | bytes 22151168
  2150.6 52.5 %copy.82 = bf16[13312,1,416]{0,2,1:T(8,128)(2,1)} copy(bf16[13312,1,416]{2,1,0:T(2,128)(2,1)} %reshape.164) | data formatting | bytes 22151168 | tf_op jit(solution)/shard_map/all_to_all | solution.py:48
  2260.6 97.7 %all-to-all-done.7 = bf16[4,2,692224]{2,1,0:T(2,128)(2,1)} async-done(((bf16[4,2,692224]{2,1,0:T(2,128)(2,1)}), bf16[4,2,692224]{2,1,0:T(2,128)(2,1)}, u32[]{:S(2)}, u32[]{:S(2)}) %all-to-all-start.7) | async-done | bytes 11075616 | tf_op jit(solution)/shard_map/all_to_all | solution.py:54
  2358.3 45.3 %reshape.166 = bf16[13312,1,416]{2,1,0:T(2,128)(2,1)} reshape(bf16[4,2,692224]{2,1,0:T(2,128)(2,1)} %all-to-all-done.7) | data formatting | bytes 22151168
  2403.6 52.7 %copy.88 = bf16[13312,1,416]{0,2,1:T(8,128)(2,1)} copy(bf16[13312,1,416]{2,1,0:T(2,128)(2,1)} %reshape.166) | data formatting | bytes 22151168 | tf_op jit(solution)/shard_map/all_to_all | solution.py:54
  2497.2 40.2 %multiply_reduce_fusion.1 = (f32[]{:T(128)}, f32[]{:T(128)}, f32[1664,3328]{1,0:T(8,128)}) fusion(f32[1664,3328]{1,0:T(8,128)} %get-tuple-element.13, f32[]{:T(128)S(6)} %max.13, bf16[1664,3328]{1,0:T(8,128)(2,1)} %param.5, f32[]{:T(128)} %sqrt.10, f32[1664,3328]{1,0:T(8,128)} %get-tuple-element.15, f32[1664,3328]{1,0:T(8,128)} %copy.90, ...), kind=kLoop, calls=%fused_computation.18 | loop fusion | flops 66453504 | bytes 121831440 | tf_op jit(solution)/shard_map/reduce_sum | solution.py:62
  2537.4 42.5 %all-reduce = (f32[]{:T(128)}, f32[]{:T(128)}) all-reduce(f32[]{:T(128)} %get-tuple-element.4, f32[]{:T(128)} %get-tuple-element.3), channel_id=1, replica_groups=mesh['up'=8,'dn'=4] {'up','dn'}, use_global_device_ids=true, to_apply=%region_9.0 | all-reduce | flops 2 | bytes 16 | tf_op jit(solution)/shard_map/psum | solution.py:62
  (69 shorter events, 727.4 us)
Async XLA Ops:
  80.3 133.9 %copy-start.4 = (s32[104,5]{0,1:T(8,128)S(1)}, s32[104,5]{0,1:T(8,128)}, u32[]{:S(2)}) copy-start(s32[104,5]{0,1:T(8,128)} %param.8) | copy-start | bytes 6244
  80.3 134.0 %copy-start.5 = (s32[104,5]{0,1:T(8,128)S(1)}, s32[104,5]{0,1:T(8,128)}, u32[]{:S(2)}) copy-start(s32[104,5]{0,1:T(8,128)} %param.7) | copy-start | bytes 6244
  207.5 317.4 %all-to-all-start.2 = ((bf16[3328,4,416]{0,2,1:T(8,128)(2,1)}), bf16[3328,4,416]{0,2,1:T(8,128)(2,1)}, u32[]{:S(2)}, u32[]{:S(2)}) async-start(bf16[3328,4,416]{0,2,1:T(8,128)(2,1)} %bitcast.96), calls=%async_computation.2 | async-start | bytes 22151168 | tf_op jit(solution)/shard_map/all_to_all | solution.py:51
  214.3 399.5 %copy-start.2 = (bf16[104,5]{1,0:T(8,128)(2,1)}, bf16[104,5]{1,0:T(8,128)(2,1)S(1)}, u32[]{:S(2)}) copy-start(bf16[104,5]{1,0:T(8,128)(2,1)S(1)} %copy.61) | copy-start | bytes 3124
  214.7 372.7 %copy-start = (s32[1024]{0:T(1024)}, s32[1024]{0:T(1024)S(1)}, u32[]{:S(2)}) copy-start(s32[1024]{0:T(1024)S(1)} %pad_clamp_fusion) | copy-start | bytes 12292
  524.9 322.3 %all-to-all-start.1 = ((bf16[8,2,346112]{2,1,0:T(2,128)(2,1)}), bf16[8,2,346112]{2,1,0:T(2,128)(2,1)}, u32[]{:S(2)}, u32[]{:S(2)}) async-start(bf16[8,2,346112]{2,1,0:T(2,128)(2,1)} %reshape.159), calls=%async_computation.1 | async-start | bytes 22151168 | tf_op jit(solution)/shard_map/all_to_all | solution.py:48
  847.2 244.5 %all-to-all-start.3 = ((bf16[4,2,692224]{2,1,0:T(2,128)(2,1)}), bf16[4,2,692224]{2,1,0:T(2,128)(2,1)}, u32[]{:S(2)}, u32[]{:S(2)}) async-start(bf16[4,2,692224]{2,1,0:T(2,128)(2,1)} %reshape.161), calls=%async_computation.3 | async-start | bytes 22151168 | tf_op jit(solution)/shard_map/all_to_all | solution.py:54
  1475.6 315.9 %all-to-all-start.6 = ((bf16[3328,4,416]{0,2,1:T(8,128)(2,1)}), bf16[3328,4,416]{0,2,1:T(8,128)(2,1)}, u32[]{:S(2)}, u32[]{:S(2)}) async-start(bf16[3328,4,416]{0,2,1:T(8,128)(2,1)} %bitcast.97), calls=%async_computation.6 | async-start | bytes 22151168 | tf_op jit(solution)/shard_map/all_to_all | solution.py:51
  1500.6 31.8 %copy-start.1 = (s32[1024]{0:T(1024)S(1)}, s32[1024]{0:T(1024)}, u32[]{:S(2)}) copy-start(s32[1024]{0:T(1024)} %copy-done) | copy-start | bytes 12292
  1532.4 26.5 %copy-start.3 = (bf16[104,5]{1,0:T(8,128)(2,1)S(1)}, bf16[104,5]{1,0:T(8,128)(2,1)}, u32[]{:S(2)}) copy-start(bf16[104,5]{1,0:T(8,128)(2,1)} %copy-done.2) | copy-start | bytes 3124
  1791.6 322.3 %all-to-all-start.5 = ((bf16[8,2,346112]{2,1,0:T(2,128)(2,1)}), bf16[8,2,346112]{2,1,0:T(2,128)(2,1)}, u32[]{:S(2)}, u32[]{:S(2)}) async-start(bf16[8,2,346112]{2,1,0:T(2,128)(2,1)} %reshape.163), calls=%async_computation.5 | async-start | bytes 22151168 | tf_op jit(solution)/shard_map/all_to_all | solution.py:48
  2113.8 244.5 %all-to-all-start.7 = ((bf16[4,2,692224]{2,1,0:T(2,128)(2,1)}), bf16[4,2,692224]{2,1,0:T(2,128)(2,1)}, u32[]{:S(2)}, u32[]{:S(2)}) async-start(bf16[4,2,692224]{2,1,0:T(2,128)(2,1)} %reshape.165), calls=%async_computation.7 | async-start | bytes 22151168 | tf_op jit(solution)/shard_map/all_to_all | solution.py:54
where the time goes:
time: 2630 us; the launch traced here: 2610 us
  local copies, waits for them, and re-layouts  1360 us (52%)
  other arithmetic  469 us (18%)
  blocking collectives  381 us (14%)
  waiting for transfers between devices  194 us (7%)
  matrix products  150 us (6%)
  starting transfers between devices  39.6 us (2%)
    convert_element_type x9, local copies, waits for them, and re-layouts, hop_lead(): return result.reshape(layout).astype(jnp.bfloat16)  376 us
    convert_element_type x4, other arithmetic, hop_lead(): return result.reshape(layout).astype(jnp.bfloat16)  350 us
    unnamed x22, local copies, waits for them, and re-layouts  257 us
    all_to_all x2, blocking collectives, body(): lax.all_to_all(cube, 'up', split_axis=1, concat_axis=0, tiled=True)  254 us
    all_to_all x2, waiting for transfers between devices, body(): lax.all_to_all(hopped, 'dn', split_axis=0, concat_axis=1, tiled=True)  194 us
    another operation x8, local copies, waits for them, and re-layouts, hop_lead(): cube = matrix.reshape(layout[0] // tile_width, tile_width, -1)  122 us
    dot_general x4, matrix products, hop_lead(): jnp.einsum('ikab,ikbm->iam', signed, picked, preferred_element_type=jnp.f...  118 us
    gather x4, local copies, waits for them, and re-layouts, hop_lead(): picked = cube[tile_columns]  106 us
  transfers between devices with their start and end apart: 6, of which 2 were waited for; matrix products, arithmetic and copies ran while one was open for 59% of the time, Pallas kernels for 0%

commit v1 on v0

v1 whole, which is shorter than its diff:
```python
import functools

import jax
import jax.numpy as jnp
from jax import lax
from jax.experimental import pallas as pl
from jax.experimental.pallas import tpu as pltpu
from jax.sharding import PartitionSpec as P

STEPS = 2


coupling = 4.0


def hop_kernel(tile_k, tile, group, parts_tiles, columns_ref, x_ref, tiles_ref, out_ref):
    first = pl.program_id(0) * group

    def one_tile(t, carry):
        picked = []
        for k in range(tile_k):
            column = columns_ref[(first + t) * tile_k + k]
            at = pl.multiple_of(lax.rem(column, parts_tiles) * tile, tile)
            picked.append(x_ref[lax.div(column, parts_tiles), :, pl.ds(at, tile)])
        left = jnp.concatenate(picked, axis=1)
        result = jnp.dot(left, tiles_ref[t], preferred_element_type=jnp.float32)
        out_ref[0, :, pl.ds(pl.multiple_of(t * tile, tile), tile)] = result.astype(jnp.bfloat16)
        return carry

    lax.fori_loop(0, group, one_tile, 0)


def hop_blocks(x, stacked, columns, tile_k):
    parts, rows, width = x.shape
    tiles, depth, tile = stacked.shape
    if width % tile:
        joined = x.transpose(1, 0, 2).reshape(1, rows, parts * width)
        hopped = hop_blocks(joined, stacked, columns, tile_k)
        return hopped.reshape(rows, parts, width).transpose(1, 0, 2)
    parts_tiles = width // tile
    group = max(d for d in range(1, 17) if parts_tiles % d == 0)
    per_part = parts_tiles // group
    return pl.pallas_call(
        functools.partial(hop_kernel, tile_k, tile, group, parts_tiles),
        grid_spec=pltpu.PrefetchScalarGridSpec(
            num_scalar_prefetch=1,
            grid=(tiles // group,),
            in_specs=[
                pl.BlockSpec((parts, rows, width), lambda i, c: (0, 0, 0)),
                pl.BlockSpec((group, depth, tile), lambda i, c: (i, 0, 0)),
            ],
            out_specs=pl.BlockSpec(
                (1, rows, group * tile), lambda i, c: (i // per_part, 0, i % per_part)
            ),
        ),
        out_shape=jax.ShapeDtypeStruct(x.shape, jnp.bfloat16),
        compiler_params=pltpu.CompilerParams(vmem_limit_bytes=56 * 1024 * 1024),
        cost_estimate=pl.CostEstimate(
            flops=2 * rows * tiles * depth * tile,
            bytes_accessed=4 * rows * parts * width + 2 * tiles * depth * tile,
            transcendentals=0,
        ),
    )(columns, x, stacked)


def body(start_vector, hop_tiles, tile_columns, tile_signs, occupation):
    tiles, tile_k, tile, _ = hop_tiles.shape
    signed = hop_tiles * (1 - 2 * tile_signs).astype(jnp.bfloat16)[:, :, None, None]
    stacked = signed.transpose(0, 1, 3, 2).reshape(tiles, tile_k * tile, tile)
    columns = tile_columns.reshape(-1)
    block_rows, block_cols = start_vector.shape
    count_up = lax.axis_size("up")
    count_down = lax.axis_size("dn")
    row_start = lax.axis_index("up") * block_rows
    col_start = lax.axis_index("dn") * block_cols
    occ_rows = lax.dynamic_slice_in_dim(occupation, row_start, block_rows, 1).astype(jnp.bfloat16)
    occ_cols = lax.dynamic_slice_in_dim(occupation, col_start, block_cols, 1).astype(jnp.bfloat16)
    diagonal = (
        coupling * jnp.einsum("sa,sb->ab", occ_rows, occ_cols, preferred_element_type=jnp.float32)
    ).astype(jnp.bfloat16)
    total = lax.psum(jnp.sum(jnp.square(start_vector.astype(jnp.float32))), ("up", "dn"))
    scale = 1.0 / jnp.maximum(jnp.sqrt(total), 1.0)
    vector = start_vector.astype(jnp.float32) * scale
    length = total / jnp.maximum(total, 1.0)
    previous = None
    beta_value = None
    alpha_list = []
    beta_list = []
    for iteration in range(STEPS):
        rounded = start_vector if iteration == 0 else vector.astype(jnp.bfloat16)
        down = rounded.reshape(count_down, block_rows // count_down, block_cols)
        up = rounded.T.reshape(count_up, block_cols // count_up, block_rows)
        down = lax.all_to_all(down, "dn", 0, 0, tiled=True)
        up = lax.all_to_all(up, "up", 0, 0, tiled=True)
        down = hop_blocks(down, stacked, columns, tile_k)
        down = lax.all_to_all(down, "dn", 0, 0, tiled=True)
        up = hop_blocks(up, stacked, columns, tile_k)
        up = lax.all_to_all(up, "up", 0, 0, tiled=True)
        hopped_down = down.reshape(block_rows, block_cols)
        hopped_up = up.reshape(block_cols, block_rows).T
        hopped = hopped_up.astype(jnp.float32) + hopped_down.astype(jnp.float32)
        if iteration == 0:
            work = hopped * scale + diagonal * vector
        else:
            work = hopped + diagonal * vector - beta_value * previous
        intersect, square = lax.psum((jnp.sum(work * vector), jnp.sum(work * work)), ("up", "dn"))
        work = work - intersect * vector
        residual = square - 2.0 * intersect * intersect + intersect * intersect * length
        beta_value = jnp.sqrt(jnp.maximum(residual, 1.0))
        length = residual / jnp.maximum(residual, 1.0)
        previous = vector
        vector = work / beta_value
        alpha_list.append(intersect)
        beta_list.append(beta_value)
    final = vector.astype(jnp.bfloat16)
    return (final, jnp.stack(alpha_list), jnp.stack(beta_list))


def solution(mesh):
    placed = (P("up", "dn"), P(), P(), P(), P())
    return jax.shard_map(
        body, mesh=mesh, in_specs=placed, out_specs=(P("up", "dn"), P(), P()), check_vma=False
    )
```

time: 2630 us -> 1790 us (0.68)
  local copies, waits for them, and re-layouts: 1360 us -> 103 us
  waiting for transfers between devices: 194 us -> 726 us
  other arithmetic: 469 us -> 134 us
  blocking collectives: 381 us -> 591 us
  Pallas kernels: 0 us -> 155 us
  matrix products: 150 us -> 22.9 us
    all_to_all x6, waiting for transfers between devices: 194 us -> 726 us  [the longest x4 561 us: body(): down = lax.all_to_all(down, 'dn', 0, 0, tiled=True)]
    convert_element_type x19 -> x2, local copies, waits for them, and re-layouts: 575 us -> 45.6 us  [body(): hopped = hopped_up.astype(jnp.float32) + hopped_down.astype(jnp.float32)]
    convert_element_type x8 -> x3, other arithmetic: 397 us -> 53.9 us  [the longest x1 29.5 us: body(): rounded = start_vector if iteration == 0 else vector.astype(jnp.bfloat16)]
    all_to_all x8 -> x0, local copies, waits for them, and re-layouts: 300 us -> none  [the longest x2 106 us: body(): lax.all_to_all(hopped, 'dn', split_axis=0, concat_axis=1, tiled=True)]
    unnamed x22 -> x5, local copies, waits for them, and re-layouts: 257 us -> 0.11 us
    psum x1, blocking collectives: 41.6 us -> 249 us  [body(): lax.psum(jnp.sum(jnp.square(start_vector.astype(jnp.float32))), ('up', 'd...]
    pallas_call x0 -> x4, Pallas kernels: none -> 155 us  [hop_blocks(): pl.pallas_call(functools.partial(hop_kernel, tile_k, tile, group, parts_t...]
    another operation x8 -> x0, local copies, waits for them, and re-layouts: 122 us -> none  [hop_lead(): cube = matrix.reshape(layout[0] // tile_width, tile_width, -1)]
  transfers between devices with their start and end apart: 6 -> 6, of which waited for: 2 -> 5; matrix products, arithmetic and copies ran while one was open for 59% -> 7% of each run, Pallas kernels for 0% -> 9%
where the time goes in v1:
time: 1790 us
  waiting for transfers between devices  726 us (41%)
  blocking collectives  591 us (33%)
  Pallas kernels  155 us (9%)
  other arithmetic  134 us (7%)
  local copies, waits for them, and re-layouts  103 us (6%)
  starting transfers between devices  43.9 us (2%)
  matrix products  22.9 us (1%)
    all_to_all x4, waiting for transfers between devices, body(): down = lax.all_to_all(down, 'dn', 0, 0, tiled=True)  561 us
    all_to_all x2, blocking collectives, body(): up = lax.all_to_all(up, 'up', 0, 0, tiled=True)  255 us
    psum x1, blocking collectives, body(): lax.psum(jnp.sum(jnp.square(start_vector.astype(jnp.float32))), ('up', 'd...  249 us
    all_to_all x2, waiting for transfers between devices, body(): up = lax.all_to_all(up, 'up', 0, 0, tiled=True)  165 us
    pallas_call x4, Pallas kernels, hop_blocks(): pl.pallas_call(functools.partial(hop_kernel, tile_k, tile, group, parts_t...  155 us
    psum x2, blocking collectives, body(): lax.psum((jnp.sum(work * vector), jnp.sum(work * work)), ('up', 'dn'))  86.9 us
    convert_element_type x2, local copies, waits for them, and re-layouts, body(): hopped = hopped_up.astype(jnp.float32) + hopped_down.astype(jnp.float32)  45.6 us
  transfers between devices with their start and end apart: 6, of which 5 were waited for; matrix products, arithmetic and copies ran while one was open for 7% of the time, Pallas kernels for 9%

profile of v1, /device:TPU:12, one launch (start us, length us, event | category | flops | bytes accessed | tf_op | source)
XLA Modules:
  0.0 1785.3 jit_solution(8246984403498989128)
XLA Ops:
  0.6 17.2 copy.15
  17.9 128.1 %all_to_all.40.x_ref = bf16[8,416,1664]{2,1,0:T(8,128)(2,1)} all-to-all(bf16[8,416,1664]{2,1,0:T(8,128)(2,1)} %bitcast.53), channel_id=1, replica_groups=mesh['up'=8,'dn'=4] {'up'}, dimensions={0} | all-to-all | bytes 22151168 | tf_op jit(solution)/shard_map/all_to_all | solution.py:94
  145.9 6.1 all-to-all-start.2
  153.1 14.1 multiply_bitcast_fusion
  167.2 22.7 %copy.17 = bf16[104,5,128,128]{3,2,1,0:T(8,128)(2,1)} copy(bf16[104,5,128,128]{2,3,1,0:T(8,128)(2,1)} %multiply_bitcast_fusion) | data formatting | bytes 34078720 | tf_op jit(solution)/shard_map/transpose | solution.py:69
  189.9 38.8 %shard_map.76 = bf16[8,416,1664]{2,1,0:T(8,128)(2,1)} custom-call(s32[520]{0:T(1024)} %reshape.37.columns_ref, bf16[8,416,1664]{2,1,0:T(8,128)(2,1)} %all_to_all.40.x_ref, bf16[104,640,128]{2,1,0:T(8,128)(2,1)} %bitcast.45), custom_call_target="tpu_custom_call" | custom-call | flops 7088373760 | bytes 39190528 | tf_op jit(solution)/shard_map/pallas_call | solution.py:43
  228.7 161.3 %all-to-all-done.2.x_ref = bf16[4,416,3328]{2,1,0:T(8,128)(2,1)} async-done(((bf16[4,416,3328]{2,1,0:T(8,128)(2,1)}), bf16[4,416,3328]{2,1,0:T(8,128)(2,1)}, u32[]{:S(2)}, u32[]{:S(2)}) %all-to-all-start.2) | async-done | bytes 11075616 | tf_op jit(solution)/shard_map/all_to_all | solution.py:93
  389.9 6.5 all-to-all-start.1
  396.4 38.9 %shard_map.77 = bf16[4,416,3328]{2,1,0:T(8,128)(2,1)} custom-call(s32[520]{0:T(1024)} %reshape.37.columns_ref, bf16[4,416,3328]{2,1,0:T(8,128)(2,1)} %all-to-all-done.2.x_ref, bf16[104,640,128]{2,1,0:T(8,128)(2,1)} %bitcast.46), custom_call_target="tpu_custom_call" | custom-call | flops 7088373760 | bytes 39190528 | tf_op jit(solution)/shard_map/pallas_call | solution.py:43
  435.3 82.5 %all-to-all-done.1 = bf16[8,416,1664]{2,1,0:T(8,128)(2,1)} async-done(((bf16[8,416,1664]{2,1,0:T(8,128)(2,1)}), bf16[8,416,1664]{2,1,0:T(8,128)(2,1)}, u32[]{:S(2)}, u32[]{:S(2)}) %all-to-all-start.1) | async-done | bytes 11075616 | tf_op jit(solution)/shard_map/all_to_all | solution.py:98
  517.8 9.5 all-to-all-start.3
  527.3 10.4 fusion.7
  537.8 248.7 %psum.35 = f32[]{:T(128)} all-reduce(f32[]{:T(128)} %fusion.7), channel_id=1, replica_groups=mesh['up'=8,'dn'=4] {'up','dn'}, use_global_device_ids=true, to_apply=%region_1.0 | all-reduce | flops 1 | bytes 8 | tf_op jit(solution)/shard_map/psum | solution.py:81
  788.5 12.2 bitcast_convert_fusion.1
  800.7 22.8 %copy.18 = f32[3328,1664]{0,1:T(8,128)} copy(f32[3328,1664]{1,0:T(8,128)} %bitcast_convert_fusion.1) | data formatting | bytes 44302336 | tf_op jit(solution)/shard_map/convert_element_type | solution.py:101
  823.5 22.9 %fusion.3 = (f32[]{:T(128)}, f32[]{:T(128)}, bf16[1664,3328]{1,0:T(8,128)(2,1)}) fusion(bf16[1664,3328]{1,0:T(8,128)(2,1)} %param.5, f32[]{:T(128)S(6)} %div.21, bf16[4,416,3328]{2,1,0:T(8,128)(2,1)} %all-to-all-done.3, f32[3328,1664]{0,1:T(8,128)} %copy.18, s32[16,13312]{1,0:T(8,128)} %param.9, s32[]{:T(128)S(6)} %select_n.7, s32[]{:T(128)S(6)} %select_n.6), kind=kOutput, calls=%fused_computation.7 | convolution fusion | flops 254818304 | bytes 55697428 | tf_op jit(solution)/shard_map/sa,sb->ab/dot_general | solution.py:79
  846.5 42.4 %all-reduce.1 = (f32[]{:T(128)}, f32[]{:T(128)}) all-reduce(f32[]{:T(128)} %get-tuple-element.4, f32[]{:T(128)} %get-tuple-element.3), channel_id=1, replica_groups=mesh['up'=8,'dn'=4] {'up','dn'}, use_global_device_ids=true, to_apply=%region_5.0 | all-reduce | flops 2 | bytes 16 | tf_op jit(solution)/shard_map/psum | solution.py:106
  892.4 29.5 %fusion.13 = (bf16[1664,3328]{1,0:T(8,128)(2,1)}, f32[1664,3328]{1,0:T(8,128)}) fusion(f32[]{:T(128)} %sqrt.10, f32[]{:T(128)} %get-tuple-element.10, bf16[1664,3328]{1,0:T(8,128)(2,1)} %param.5, bf16[1664,3328]{1,0:T(8,128)(2,1)} %get-tuple-element.14, f32[]{:T(128)S(6)} %div.21, bf16[4,416,3328]{2,1,0:T(8,128)(2,1)} %all-to-all-done.3, f32[3328,1664]{0,1:T(8,128)} %copy.18), kind=kLoop, calls=%fused_computation.31 | loop fusion | flops 66453504 | bytes 88604688 | tf_op jit(solution)/shard_map/convert_element_type | solution.py:90
  921.9 16.3 copy.19
  938.2 127.0 %all_to_all.41.x_ref = bf16[8,416,1664]{2,1,0:T(8,128)(2,1)} all-to-all(bf16[8,416,1664]{2,1,0:T(8,128)(2,1)} %bitcast.54), channel_id=1, replica_groups=mesh['up'=8,'dn'=4] {'up'}, dimensions={0} | all-to-all | bytes 22151168 | tf_op jit(solution)/shard_map/all_to_all | solution.py:94
  1071.2 38.7 %shard_map.78 = bf16[8,416,1664]{2,1,0:T(8,128)(2,1)} custom-call(s32[520]{0:T(1024)} %reshape.37.columns_ref, bf16[8,416,1664]{2,1,0:T(8,128)(2,1)} %all_to_all.41.x_ref, bf16[104,640,128]{2,1,0:T(8,128)(2,1)} %bitcast.47), custom_call_target="tpu_custom_call" | custom-call | flops 7088373760 | bytes 39190528 | tf_op jit(solution)/shard_map/pallas_call | solution.py:43
  1110.0 199.1 %all-to-all-done.6.x_ref = bf16[4,416,3328]{2,1,0:T(8,128)(2,1)} async-done(((bf16[4,416,3328]{2,1,0:T(8,128)(2,1)}), bf16[4,416,3328]{2,1,0:T(8,128)(2,1)}, u32[]{:S(2)}, u32[]{:S(2)}) %all-to-all-start.6) | async-done | bytes 11075616 | tf_op jit(solution)/shard_map/all_to_all | solution.py:93
  1309.1 6.5 all-to-all-start.5
  1315.6 39.0 %shard_map.79 = bf16[4,416,3328]{2,1,0:T(8,128)(2,1)} custom-call(s32[520]{0:T(1024)} %reshape.37.columns_ref, bf16[4,416,3328]{2,1,0:T(8,128)(2,1)} %all-to-all-done.6.x_ref, bf16[104,640,128]{2,1,0:T(8,128)(2,1)} %bitcast.48), custom_call_target="tpu_custom_call" | custom-call | flops 7088373760 | bytes 39190528 | tf_op jit(solution)/shard_map/pallas_call | solution.py:43
  1354.6 82.5 %all-to-all-done.5 = bf16[8,416,1664]{2,1,0:T(8,128)(2,1)} async-done(((bf16[8,416,1664]{2,1,0:T(8,128)(2,1)}), bf16[8,416,1664]{2,1,0:T(8,128)(2,1)}, u32[]{:S(2)}, u32[]{:S(2)}) %all-to-all-start.5) | async-done | bytes 11075616 | tf_op jit(solution)/shard_map/all_to_all | solution.py:98
  1437.0 9.3 all-to-all-start.7
  1446.4 12.2 bitcast_convert_fusion
  1458.6 22.8 %copy.20 = f32[3328,1664]{0,1:T(8,128)} copy(f32[3328,1664]{1,0:T(8,128)} %bitcast_convert_fusion) | data formatting | bytes 44302336 | tf_op jit(solution)/shard_map/convert_element_type | solution.py:101
  1481.5 200.4 %all-to-all-done.7 = bf16[4,416,3328]{2,1,0:T(8,128)(2,1)} async-done(((bf16[4,416,3328]{2,1,0:T(8,128)(2,1)}), bf16[4,416,3328]{2,1,0:T(8,128)(2,1)}, u32[]{:S(2)}, u32[]{:S(2)}) %all-to-all-start.7) | async-done | bytes 11075616 | tf_op jit(solution)/shard_map/all_to_all | solution.py:96
  1681.8 34.1 %multiply_reduce_fusion.1 = (f32[]{:T(128)}, f32[]{:T(128)}, f32[1664,3328]{1,0:T(8,128)}) fusion(f32[1664,3328]{1,0:T(8,128)} %get-tuple-element.13, f32[]{:T(128)S(6)} %div.21, bf16[1664,3328]{1,0:T(8,128)(2,1)} %param.5, f32[]{:T(128)} %sqrt.10, bf16[1664,3328]{1,0:T(8,128)(2,1)} %get-tuple-element.14, bf16[4,416,3328]{2,1,0:T(8,128)(2,1)} %all-to-all-done.7, ...), kind=kLoop, calls=%fused_computation.19 | loop fusion | flops 71991296 | bytes 99680272 | tf_op jit(solution)/shard_map/reduce_sum | solution.py:106
  1715.9 44.5 %all-reduce = (f32[]{:T(128)}, f32[]{:T(128)}) all-reduce(f32[]{:T(128)} %get-tuple-element.6, f32[]{:T(128)} %get-tuple-element.5), channel_id=1, replica_groups=mesh['up'=8,'dn'=4] {'up','dn'}, use_global_device_ids=true, to_apply=%region_9.0 | all-reduce | flops 2 | bytes 16 | tf_op jit(solution)/shard_map/psum | solution.py:106
  1763.8 19.5 %divide_convert_fusion = bf16[1664,3328]{1,0:T(8,128)(2,1)} fusion(f32[1664,3328]{1,0:T(8,128)} %get-tuple-element.11, f32[1664,3328]{1,0:T(8,128)} %get-tuple-element.13, f32[]{:T(128)} %sqrt.11, f32[]{:T(128)} %get-tuple-element.8), kind=kLoop, calls=%fused_computation.17 | loop fusion | flops 22151168 | bytes 55377928 | tf_op jit(solution)/shard_map/convert_element_type | solution.py:115
  (11 shorter events, 9.0 us)
Async XLA Ops:
  17.8 134.2 %copy-start.1 = (s32[104,5]{0,1:T(8,128)S(1)}, s32[104,5]{0,1:T(8,128)}, u32[]{:S(2)}) copy-start(s32[104,5]{0,1:T(8,128)} %param.8) | copy-start | bytes 6244
  17.9 134.3 %copy-start = (s32[104,5]{0,1:T(8,128)S(1)}, s32[104,5]{0,1:T(8,128)}, u32[]{:S(2)}) copy-start(s32[104,5]{0,1:T(8,128)} %param.7) | copy-start | bytes 6244
  145.9 244.0 %all-to-all-start.2 = ((bf16[4,416,3328]{2,1,0:T(8,128)(2,1)}), bf16[4,416,3328]{2,1,0:T(8,128)(2,1)}, u32[]{:S(2)}, u32[]{:S(2)}) async-start(bf16[4,416,3328]{2,1,0:T(8,128)(2,1)} %bitcast.50), calls=%async_computation.2 | async-start | bytes 22151168 | tf_op jit(solution)/shard_map/all_to_all | solution.py:93
  389.9 127.9 %all-to-all-start.1 = ((bf16[8,416,1664]{2,1,0:T(8,128)(2,1)}), bf16[8,416,1664]{2,1,0:T(8,128)(2,1)}, u32[]{:S(2)}, u32[]{:S(2)}) async-start(bf16[8,416,1664]{2,1,0:T(8,128)(2,1)} %shard_map.76), calls=%async_computation.1 | async-start | bytes 22151168 | tf_op jit(solution)/shard_map/all_to_all | solution.py:98
  517.8 305.7 %all-to-all-start.3 = ((bf16[4,416,3328]{2,1,0:T(8,128)(2,1)}), bf16[4,416,3328]{2,1,0:T(8,128)(2,1)}, u32[]{:S(2)}, u32[]{:S(2)}) async-start(bf16[4,416,3328]{2,1,0:T(8,128)(2,1)} %shard_map.77), calls=%async_computation.3 | async-start | bytes 22151168 | tf_op jit(solution)/shard_map/all_to_all | solution.py:96
  1065.2 244.0 %all-to-all-start.6 = ((bf16[4,416,3328]{2,1,0:T(8,128)(2,1)}), bf16[4,416,3328]{2,1,0:T(8,128)(2,1)}, u32[]{:S(2)}, u32[]{:S(2)}) async-start(bf16[4,416,3328]{2,1,0:T(8,128)(2,1)} %bitcast.52), calls=%async_computation.6 | async-start | bytes 22151168 | tf_op jit(solution)/shard_map/all_to_all | solution.py:93
  1309.1 127.9 %all-to-all-start.5 = ((bf16[8,416,1664]{2,1,0:T(8,128)(2,1)}), bf16[8,416,1664]{2,1,0:T(8,128)(2,1)}, u32[]{:S(2)}, u32[]{:S(2)}) async-start(bf16[8,416,1664]{2,1,0:T(8,128)(2,1)} %shard_map.78), calls=%async_computation.5 | async-start | bytes 22151168 | tf_op jit(solution)/shard_map/all_to_all | solution.py:98
  1437.0 244.8 %all-to-all-start.7 = ((bf16[4,416,3328]{2,1,0:T(8,128)(2,1)}), bf16[4,416,3328]{2,1,0:T(8,128)(2,1)}, u32[]{:S(2)}, u32[]{:S(2)}) async-start(bf16[4,416,3328]{2,1,0:T(8,128)(2,1)} %shard_map.79), calls=%async_computation.7 | async-start | bytes 22151168 | tf_op jit(solution)/shard_map/all_to_all | solution.py:96
